TPU v7x, 128 devices: a whole 4x4x4 slice. The times are simulated.
128 devices in a mesh: tm: 128 (over x, z, y, core).
Axes of the slice: x: 4, y: 4, z: 4, core: 2. Of those that a mesh axis runs over, the one named last changes fastest.
Arguments:
- field: bfloat16 [43008, 8192], P('tm'), may hold values from -52 to 52
- index: float32 [43008, 10], P('tm'), may hold values from -13 to 13
- lag_list: int32 [61], replicated, may hold values from -30 to 30, as said below
- index_offset: int32 [10], replicated, may hold values from 0 to 14, as said below
- sea_mask: int32 [8192], P('tm'), may hold values 0 or 1
Outputs:
- corr_maps: float32 [8192, 10, 61], P('tm')
Inputs may be any that keep to these rules, and one draw needn't show every extreme that they name: `lag_list`: each whole number of -30 to 30 appears once. `index_offset`: some index has the extra lead 14.
All inputs are finite; a program needn't handle non-finite values. No bound on the sum of `sea_mask` on one device may be relied on, other than what follows from the above.
Results may differ from a plain program's by a relative error of at most 0.00051.
Values may be sent and summed in bfloat16 or wider, within the bound.
No kernel may reach another device: no remote copies, remote signals or barrier semaphores. Data moves between devices by JAX's collectives and lax.ppermute only.
A program may use at most 256 MiB of HBM per device.

v0:
```python
import jax
import jax.numpy as jnp
from jax import lax
from jax.experimental import pallas as pl
from jax.experimental.pallas import tpu as pltpu
from jax.sharding import PartitionSpec as P

TM = "tm"
CORES = 2
WEIGHTS = (1, 16, 4)
DIGITS = ((3, 2, 1, 0), (3, 2, 1, 0), (2, 3, 0, 1))
PHASES = 6
KCOUNT = 10
USED = PHASES * KCOUNT
LANES = 128
HALF = 64
BEFORE = 8
TILES = 7
WIDTH = TILES * LANES
SUM_LANE = BEFORE * HALF + USED
SQUARE_LANE = SUM_LANE + 1
ROWS = HALF + 16
STEP = 8
EARLY = 32
F32 = jnp.float32
BF16 = jnp.bfloat16
VMEM = pl.BlockSpec(memory_space=pltpu.VMEM)
ANY = pl.BlockSpec(memory_space=pl.ANY)
SMALL = pltpu.CompilerParams(vmem_limit_bytes=8 << 20)


def chip_at(place):
    chip = 0
    for i, (weight, digits) in enumerate(zip(WEIGHTS, DIGITS)):
        digit = (place >> (4 - 2 * i)) & 3
        table = sum(value << (2 * at) for at, value in enumerate(digits))
        chip = chip + weight * ((table >> (2 * digit)) & 3)
    return chip


def local(array):
    return pltpu.with_memory_space_constraint(array, pltpu.VMEM)


def fill_order(early, late):
    for target in (early, late):
        days = target.shape[0]
        length = days // PHASES
        row = lax.broadcasted_iota(jnp.int32, (length, days), 0)
        column = lax.broadcasted_iota(jnp.int32, (length, days), 1)
        for r in range(PHASES):
            target[r * length : (r + 1) * length, :] = (column == row * PHASES + r).astype(BF16)


def order_scratch(t_dev):
    ahead = EARLY * PHASES
    return [pltpu.VMEM((ahead, ahead), BF16), pltpu.VMEM((t_dev - ahead, t_dev - ahead), BF16)]


def pack_kernel(field_ref, index_ref, sent_ref, index, early, late, sems, index_sem):
    kcount, t_dev = index_ref.shape
    count = t_dev // PHASES
    chips = sent_ref.shape[0]
    ahead = EARLY * PHASES
    index_copy = pltpu.make_async_copy(index_ref, index, index_sem)
    index_copy.start()

    def copy(place):
        lanes = pl.ds(pl.multiple_of(chip_at(place) * LANES, LANES), LANES)
        return pltpu.make_async_copy(
            field_ref.at[:, lanes], sent_ref.at[place, 0:t_dev, :], sems.at[place]
        )

    def start(place, _):
        copy(place).start()
        return 0

    lax.fori_loop(0, chips, start, 0, unroll=8)
    fill_order(early, late)
    index_copy.wait()
    value = index[...]
    upper = value.astype(BF16)
    lower = (value - upper.astype(F32)).astype(BF16)
    pieces = []
    for part in (upper, lower):
        first = lax.dot_general(
            early[...], part[:, :ahead], (((1,), (1,)), ((), ())), preferred_element_type=F32
        )
        second = lax.dot_general(
            late[...], part[:, ahead:], (((1,), (1,)), ((), ())), preferred_element_type=F32
        )
        for r in range(PHASES):
            pieces.append(
                jnp.concatenate(
                    [
                        first[r * EARLY : (r + 1) * EARLY],
                        second[r * (count - EARLY) : (r + 1) * (count - EARLY)],
                    ],
                    0,
                )
            )
        pieces.append(jnp.zeros((count, HALF - USED), F32))
    rows = jnp.concatenate(pieces, axis=1).astype(BF16)

    def repeat(place, _):
        sent_ref[place, t_dev:, :] = rows
        return 0

    lax.fori_loop(0, chips, repeat, 0, unroll=8)

    def finish_copy(place, _):
        copy(place).wait()
        return 0

    lax.fori_loop(0, chips, finish_copy, 0, unroll=8)


def pack(field, index):
    t_dev, cells = field.shape
    chips = cells // LANES
    return pl.pallas_call(
        pack_kernel,
        in_specs=[ANY] * 2,
        out_specs=VMEM,
        out_shape=pltpu.VMEM((chips, t_dev + t_dev // PHASES, LANES), BF16),
        scratch_shapes=[pltpu.VMEM(index.T.shape, F32)]
        + order_scratch(t_dev)
        + [pltpu.SemaphoreType.DMA((chips,)), pltpu.SemaphoreType.DMA],
        compiler_params=SMALL,
    )(*[pltpu.with_memory_space_constraint(x, pltpu.HBM) for x in (field, index.T)])


def joined(raw):
    wide = raw.astype(F32)
    return wide + pltpu.roll(wide, HALF, 1)


def summed(value):
    return jnp.sum(value.reshape(-1, 8, LANES), 0)


def take_kernel(got_ref, own_ref, edge_ref):
    chips, count, _ = own_ref.shape
    zero = jnp.zeros((8, LANES), F32)

    def body(place, sums):
        first, second = sums
        chip = chip_at(place)
        value = joined(got_ref[place, PHASES * count :, :])
        own_ref[place] = value
        edge_ref[chip, 0:8, :] = value[0:8]
        edge_ref[chip, 8:16, :] = value[count - 8 :]
        return first + summed(value), second + summed(value * value)

    first, second = lax.fori_loop(0, chips, body, (zero, zero), unroll=16)
    edge_ref[chips, 0:8, :] = first
    edge_ref[chips, 8:16, :] = second


def take_index(got, count):
    chips = got.shape[0]
    return pl.pallas_call(
        take_kernel,
        in_specs=[VMEM],
        out_specs=[VMEM] * 2,
        out_shape=[
            pltpu.VMEM((chips, count, LANES), F32),
            pltpu.VMEM((chips + 1, 16, LANES), F32),
        ],
        compiler_params=SMALL,
    )(local(got))


def middle_kernel(got_ref, days_ref, square_ref, early, late):
    chips, rows, _ = got_ref.shape
    t_dev = rows * PHASES // (PHASES + 1)
    count = t_dev // PHASES
    ahead = EARLY * PHASES
    fill_order(early, late)

    def body(pair, square):
        start = pl.multiple_of(pair * 2 * count, 16)
        for source, days, base in ((early, slice(0, ahead), 0), (late, slice(ahead, t_dev), EARLY)):
            length = source.shape[0] // PHASES
            blocks = [got_ref[2 * pair + side, days, :] for side in range(2)]
            for block in blocks:
                wide = block.astype(F32)
                square = square + jnp.sum((wide * wide).reshape(-1, 16, LANES), 0)
            mixed = jnp.dot(
                source[...], jnp.concatenate(blocks, 1), preferred_element_type=F32
            )
            for r in range(PHASES):
                piece = mixed[r * length : (r + 1) * length].astype(BF16)
                days_ref[r, pl.ds(start + base, length), :] = piece[:, :LANES]
                days_ref[r, pl.ds(start + count + base, length), :] = piece[:, LANES:]
        return square

    square_ref[...] = lax.fori_loop(0, chips // 2, body, jnp.zeros((16, LANES), F32), unroll=8)


def middle(got, t_dev):
    chips = got.shape[0]
    return pl.pallas_call(
        middle_kernel,
        in_specs=[VMEM],
        out_specs=[VMEM] * 2,
        out_shape=[
            pltpu.VMEM((PHASES, chips * t_dev // PHASES, LANES), BF16),
            pltpu.VMEM((16, LANES), F32),
        ],
        scratch_shapes=order_scratch(t_dev),
        compiler_params=SMALL,
    )(local(got))


def spread_kernel(
    own, mine_ref, other_ref, square_ref, days,
    kept_ref, passed_ref, stat_ref,
    edge, line, slid, win, acc, merged,
):
    chips, count, _ = own.shape
    core = lax.rem(lax.axis_index(TM), CORES)
    total_days = 2.0 * chips * count * PHASES
    zero = jnp.zeros((8, LANES), F32)
    sums = mine_ref[chips] + other_ref[chips]
    row = lax.broadcasted_iota(jnp.int32, (LANES, LANES), 0)
    column = lax.broadcasted_iota(jnp.int32, (LANES, LANES), 1) % HALF
    same = (row < USED) & (column < USED) & (row % KCOUNT == column % KCOUNT)
    folded = jnp.dot(
        sums, same.astype(F32), precision=lax.Precision.HIGHEST, preferred_element_type=F32
    )
    mean = jnp.sum(folded[0:8], 0, keepdims=True) / total_days
    var = jnp.sum(folded[8:16], 0, keepdims=True) / total_days - mean * mean
    stat_ref[...] = jnp.concatenate([mean, var, jnp.zeros((6, LANES), F32)], 0)
    lane = lax.broadcasted_iota(jnp.int32, (1, LANES), 1)
    valid = lane % HALF < USED

    def centered(value):
        return jnp.where(valid, (value - mean).astype(BF16).astype(F32), 0.0)

    edge[0] = jnp.broadcast_to(mean, (16, LANES))
    edge[chips + 1] = jnp.broadcast_to(mean, (16, LANES))

    def move(chip, _):
        edge[chip + 1] = other_ref[chip]
        return 0

    lax.fori_loop(0, chips, move, 0, unroll=16)

    def slide(group, sums):
        sums = list(sums)
        for side in range(8):
            place = 8 * group + side
            chip = chip_at(place)
            line[side, 0:8, :] = centered(edge[chip + core, 8:16, :])
            line[side, 8 : 8 + count, :] = jnp.where(lane == USED, 1.0, centered(own[place]))
            line[side, 8 + count :, :] = centered(edge[chip + core + 1, 0:8, :])
        for side in range(8):
            slid[side, 0 : count + 15, :] = jnp.where(
                lane < HALF, line[side, 0 : count + 15, :], line[side, 1 : count + 16, :]
            )
        start = pl.multiple_of(group * 8 * count, 16)
        for pair in range(4):
            for q in range(TILES):
                tile = jnp.concatenate(
                    [slid[2 * pair + side, 2 * q : 2 * q + count, :] for side in range(2)], 0
                )
                sums[q] = sums[q] + summed(tile)
                win[q, pl.ds(start + pair * 2 * count, 2 * count), :] = tile.astype(BF16)
        return tuple(sums)

    window_sums = lax.fori_loop(0, chips // 8, slide, (zero,) * TILES)
    acc[0:WIDTH, :] = lax.dot_general(
        jnp.concatenate([win[q] for q in range(TILES)], 1),
        jnp.concatenate([days[r] for r in range(PHASES)], 1),
        (((0,), (0,)), ((), ())),
        preferred_element_type=F32,
    )
    acc[WIDTH:, :] = jnp.zeros((HALF, PHASES * LANES), F32)
    sums_row = jnp.concatenate([jnp.sum(s, 0, keepdims=True) for s in window_sums], 1)

    def shifted(parts):
        total = parts[0]
        lanes = lax.broadcasted_iota(jnp.int32, total.shape, 1) % HALF
        for r in range(1, PHASES):
            near = pltpu.roll(parts[r], WIDTH - KCOUNT * r, 1)
            far = pltpu.roll(parts[r], WIDTH - KCOUNT * r - (HALF - USED), 1)
            total = total + jnp.where(lanes + KCOUNT * r < USED, near, far)
        return total

    squared = jnp.sum(square_ref[...], 0, keepdims=True)
    inside = lax.broadcasted_iota(jnp.int32, (LANES, LANES), 0) % HALF
    for tile in range(TILES):
        base = tile * LANES
        total = acc[base : base + LANES, 0:LANES]
        for r in range(1, PHASES):
            lanes = slice(r * LANES, (r + 1) * LANES)
            near = base + KCOUNT * r
            far = near + HALF - USED
            total = total + jnp.where(
                inside + KCOUNT * r < USED,
                acc[near : near + LANES, lanes],
                acc[far : far + LANES, lanes],
            )
        if base <= SUM_LANE < base + LANES:
            at = lax.broadcasted_iota(jnp.int32, (LANES, LANES), 0) + base
            plain = sum(acc[base : base + LANES, r * LANES : (r + 1) * LANES] for r in range(PHASES))
            total = jnp.where(at == SUM_LANE, plain, total)
            total = jnp.where(at == SQUARE_LANE, squared, total)
        merged[:, base : base + LANES] = jnp.transpose(total)
    totals = shifted([jnp.broadcast_to(sums_row, (8, WIDTH))] * PHASES)
    kept_ref[0:HALF, :] = merged[pl.ds(pl.multiple_of(core * HALF, HALF), HALF), :]
    passed_ref[0:HALF, :] = merged[pl.ds(pl.multiple_of((1 - core) * HALF, HALF), HALF), :]
    for target in (kept_ref, passed_ref):
        target[HALF : HALF + 8, :] = totals
        target[HALF + 8 :, :] = totals


def spread(own, mine, other, square, days):
    chips, count, _ = own.shape
    return pl.pallas_call(
        spread_kernel,
        in_specs=[VMEM] * 5,
        out_specs=[VMEM] * 3,
        out_shape=[
            pltpu.VMEM((ROWS, WIDTH), F32),
            pltpu.VMEM((ROWS, WIDTH), F32),
            pltpu.VMEM((8, LANES), F32),
        ],
        scratch_shapes=[
            pltpu.VMEM((chips + 2, 16, LANES), F32),
            pltpu.VMEM((8, count + 16, LANES), F32),
            pltpu.VMEM((8, count + 16, LANES), F32),
            pltpu.VMEM((TILES, chips * count, LANES), BF16),
            pltpu.VMEM((WIDTH + HALF, PHASES * LANES), F32),
            pltpu.VMEM((LANES, WIDTH), F32),
        ],
        compiler_params=pltpu.CompilerParams(vmem_limit_bytes=32 << 20),
    )(local(own), local(mine), local(other), local(square), local(days))


def finish_kernel(
    kept_ref, taken_ref, stat_ref, lag_ref, mask_ref, offset_ref, out_ref,
    base, maps, sems, *, total_days,
):
    slots = lax.broadcasted_iota(jnp.int32, (WIDTH + 16, LANES), 0) - 16
    slot = lax.broadcasted_iota(jnp.int32, (1, LANES), 1)
    group = lax.shift_right_logical(slot * 43, 8)
    place = jnp.where(slot < TILES * 2 * PHASES, HALF * group + KCOUNT * (slot - PHASES * group), -100)
    base[...] = (slots == place).astype(F32)
    value = kept_ref[...] + taken_ref[...]
    upper = value.astype(BF16)
    rest = value - upper.astype(F32)
    middle = rest.astype(BF16)
    lower = (rest - middle.astype(F32)).astype(BF16)
    mean_x = value[0:HALF, SUM_LANE : SUM_LANE + 1] / total_days
    var_x = value[0:HALF, SQUARE_LANE : SQUARE_LANE + 1] / total_days - mean_x * mean_x
    scale_x = total_days * jnp.sqrt(var_x + 1e-06)
    scale_i = jnp.sqrt(stat_ref[1:2, :] + 1e-06)
    mask = jnp.concatenate([mask_ref[...].astype(F32), jnp.zeros((1, LANES - HALF), F32)], 1)
    mask = jnp.transpose(jnp.broadcast_to(mask, (LANES, LANES)))[0:HALF, 0:1]
    lags = lag_ref.shape[1]
    lag = jnp.concatenate([lag_ref[...], jnp.zeros((1, LANES - lags), jnp.int32)], 1)
    parts = jnp.concatenate([upper, middle, lower], 0)
    copies = []
    for pair in range(KCOUNT // 2):
        picker = jnp.concatenate(
            [base[16 - k : 16 - k + WIDTH, :].astype(BF16) for k in (2 * pair, 2 * pair + 1)], 1
        )
        thirds = jnp.dot(parts, picker, preferred_element_type=F32)
        chosen = thirds[0:ROWS] + thirds[ROWS : 2 * ROWS] + thirds[2 * ROWS :]
        for side in range(2):
            k = 2 * pair + side
            part = chosen[:, side * LANES : (side + 1) * LANES]
            wanted = BEFORE * PHASES - (lag + offset_ref[:, k : k + 1])
            part = jnp.take_along_axis(
                part, jnp.broadcast_to(wanted, part.shape), axis=1, mode="promise_in_bounds"
            )
            numer = part[0:HALF] - mean_x * part[HALF : HALF + 1]
            answer = numer / (scale_x * scale_i[:, k : k + 1]) * mask
            maps[k] = answer[:, :lags]
        copy = pltpu.make_async_copy(
            maps.at[2 * pair : 2 * pair + 2], out_ref.at[2 * pair : 2 * pair + 2], sems.at[pair]
        )
        copy.start()
        copies.append(copy)
    for copy in copies:
        copy.wait()


def finish(kept, taken, stat, lag_list, index_offset, mask, total_days):
    lags = lag_list.shape[0]
    return pl.pallas_call(
        lambda *refs: finish_kernel(*refs, total_days=total_days),
        in_specs=[VMEM] * 6,
        out_specs=ANY,
        out_shape=pltpu.HBM((KCOUNT, HALF, lags), F32),
        scratch_shapes=[
            pltpu.VMEM((WIDTH + 16, LANES), F32),
            pltpu.VMEM((KCOUNT, HALF, lags), F32),
            pltpu.SemaphoreType.DMA((KCOUNT // 2,)),
        ],
        compiler_params=SMALL,
    )(
        local(kept), local(taken), local(stat), local(lag_list[None, :]), local(mask[None, :]),
        local(index_offset[None, :]),
    )


def after(got, lag_list, index_offset, sea_mask, total_days, swapped):
    t_dev = got.shape[1] * PHASES // (PHASES + 1)
    own, mine = take_index(got, t_dev // PHASES)
    other = swapped(mine)
    days, square = middle(got, t_dev)
    kept, passed, stat = spread(own, mine, other, square, days)
    taken = swapped(passed)
    maps = finish(kept, taken, stat, lag_list, index_offset, sea_mask, total_days)
    return jnp.transpose(maps, (1, 0, 2))


def shards(field, index, lag_list, index_offset, sea_mask):
    devices = lax.axis_size(TM)
    groups = [
        [CORES * chip_at(place) + core for place in range(devices // CORES)]
        for core in range(CORES)
    ]
    got = lax.all_to_all(
        pack(field, index), TM, 0, 0, axis_index_groups=groups, tiled=True
    )
    total_days = 1.0 * index.shape[0] * devices
    swap = [(i, i ^ 1) for i in range(devices)]
    return after(
        got, lag_list, index_offset, sea_mask, total_days, lambda x: lax.ppermute(x, TM, swap)
    )


def solution(mesh):
    return jax.shard_map(
        shards,
        mesh=mesh,
        in_specs=(P(TM, None), P(TM, None), P(), P(), P(TM)),
        out_specs=P(TM, None, None),
        check_vma=False,
    )
```

profile of v0, /device:TPU:1, one launch (start us, length us, event | category | flops | bytes accessed | tf_op | source)
XLA Modules:
  0.0 102.7 jit_solution(14939193689577246720)
XLA Ops:
  0.0 3.5 %shard_map.55 = bf16[64,392,128]{2,1,0:T(8,128)(2,1)S(1)} custom-call(bf16[336,8192]{1,0:T(8,128)(2,1)} %field_ref.1, f32[10,336]{1,0:T(8,128)} %bitcast.8), custom_call_target="tpu_custom_call" | custom-call | tf_op jit(solution)/shard_map/pallas_call | solution.py:121
  3.5 84.0 %all_to_all.5.got_ref = bf16[64,392,128]{2,1,0:T(8,128)(2,1)S(1)} all-to-all(bf16[64,392,128]{2,1,0:T(8,128)(2,1)S(1)} %shard_map.55), channel_id=1, replica_groups={{118,126,102,110,86,94,70,78,54,62,38,46,22,30,6,14,116,124,100,108,84,..., dimensions={0} | all-to-all | bytes 12845056 | tf_op jit(solution)/shard_map/all_to_all | solution.py:427
  87.5 0.6 shard_map.56
  88.1 1.9 %collective-permute-start = (f32[65,16,128]{2,1,0:T(8,128)S(1)}, f32[65,16,128]{2,1,0:T(8,128)S(1)}, u32[]{:S(2)}, u32[]{:S(2)}) collective-permute-start(f32[65,16,128]{2,1,0:T(8,128)S(1)} %get-tuple-element.13.mine_ref), channel_id=1, source_target_pairs={{0,1},{1,0},{2,3},{3,2},{4,5},{5,4},{6,7},{7,6},{8,9},{9,8},{10,11... | collective-permute-start | bytes 1597448 | tf_op jit(solution)/shard_map/ppermute | solution.py:433
  90.0 2.3 %shard_map.57 = (bf16[6,3584,128]{2,1,0:T(8,128)(2,1)S(1)}, f32[16,128]{1,0:T(8,128)S(1)}) custom-call(bf16[64,392,128]{2,1,0:T(8,128)(2,1)S(1)} %all_to_all.5.got_ref), custom_call_target="tpu_custom_call" | custom-call | tf_op jit(solution)/shard_map/pallas_call | solution.py:203
  92.3 0.0 copy-start
  92.3 0.0 copy-start.1
  92.3 0.0 copy-start.2
  92.3 0.0 collective-permute-done.other_ref
  92.3 7.0 %shard_map.58 = (f32[80,896]{1,0:T(8,128)S(1)}, f32[80,896]{1,0:T(8,128)S(1)}, f32[8,128]{1,0:T(8,128)S(1)}) custom-call(f32[64,56,128]{2,1,0:T(8,128)S(1)} %get-tuple-element.12.own, f32[65,16,128]{2,1,0:T(8,128)S(1)} %get-tuple-element.13.mine_ref, f32[65,16,128]{2,1,0:T(8,128)S(1)} %collective-permute-done.other_ref, ...), custom_call_target="tpu_custom_call" | custom-call | tf_op jit(solution)/shard_map/pallas_call | solution.py:321
  99.3 0.1 collective-permute-start.1
  99.4 1.6 %collective-permute-done.1.refs_1_ = f32[80,896]{1,0:T(8,128)S(1)} collective-permute-done((f32[80,896]{1,0:T(8,128)S(1)}, f32[80,896]{1,0:T(8,128)S(1)}, u32[]{:S(2)}, u32[]{:S(2)}) %collective-permute-start.1) | collective-permute-done | bytes 286752 | tf_op jit(solution)/shard_map/ppermute | solution.py:433
  101.0 0.0 copy-done
  101.0 0.0 copy-done.1
  101.0 0.0 copy-done.2
  101.0 1.7 %shard_map.59 = f32[10,64,61]{2,1,0:T(8,128)} custom-call(f32[80,896]{1,0:T(8,128)S(1)} %get-tuple-element.16.refs_0_, f32[80,896]{1,0:T(8,128)S(1)} %collective-permute-done.1.refs_1_, f32[8,128]{1,0:T(8,128)S(1)} %get-tuple-element.18.refs_2_, s32[1,61]{1,0:T(1,128)S(1)} %bitcast.5, s32[1,64]{1,0:T(1,128)S(1)} %bitcast.6, s32[1,10]{1,0:T(1,128)S(1)} %bitcast.7), custom_call_target="tpu_custom_call" | custom-call | tf_op jit(solution)/shard_map/pallas_call | solution.py:393
Async XLA Ops:
  88.1 4.2 %collective-permute-start = (f32[65,16,128]{2,1,0:T(8,128)S(1)}, f32[65,16,128]{2,1,0:T(8,128)S(1)}, u32[]{:S(2)}, u32[]{:S(2)}) collective-permute-start(f32[65,16,128]{2,1,0:T(8,128)S(1)} %get-tuple-element.13.mine_ref), channel_id=1, source_target_pairs={{0,1},{1,0},{2,3},{3,2},{4,5},{5,4},{6,7},{7,6},{8,9},{9,8},{10,11... | collective-permute-start | bytes 1597448 | tf_op jit(solution)/shard_map/ppermute | solution.py:433
  92.3 8.7 %copy-start = (s32[61]{0:T(128)S(1)}, s32[61]{0:T(128)}, u32[]{:S(2)}) copy-start(s32[61]{0:T(128)} %param.7) | copy-start | bytes 736
  92.3 8.7 %copy-start.1 = (s32[64]{0:T(128)S(1)}, s32[64]{0:T(128)}, u32[]{:S(2)}) copy-start(s32[64]{0:T(128)} %param.9) | copy-start | bytes 772
  92.3 8.7 %copy-start.2 = (s32[10]{0:T(128)S(1)}, s32[10]{0:T(128)}, u32[]{:S(2)}) copy-start(s32[10]{0:T(128)} %param.8) | copy-start | bytes 124
  99.3 1.7 %collective-permute-start.1 = (f32[80,896]{1,0:T(8,128)S(1)}, f32[80,896]{1,0:T(8,128)S(1)}, u32[]{:S(2)}, u32[]{:S(2)}) collective-permute-start(f32[80,896]{1,0:T(8,128)S(1)} %get-tuple-element.17), channel_id=1, source_target_pairs={{0,1},{1,0},{2,3},{3,2},{4,5},{5,4},{6,7},{7,6},{8,9},{9,8},{10,11... | collective-permute-start | bytes 860168 | tf_op jit(solution)/shard_map/ppermute | solution.py:433
where the time goes:
time: 103 us
  blocking collectives  84 us (82%)
  Pallas kernels  15.1 us (15%)
  starting transfers between devices  1.97 us (2%)
  waiting for transfers between devices  1.56 us (2%)
    all_to_all x1, blocking collectives, shards(): lax.all_to_all(pack(field, index), TM, 0, 0, axis_index_groups=groups, ti...  84 us
    pallas_call x1, Pallas kernels, spread(): pl.pallas_call(spread_kernel, in_specs=[VMEM] * 5, out_specs=[VMEM] * 3,...  7.02 us
    pallas_call x1, Pallas kernels, pack(): pl.pallas_call(pack_kernel, in_specs=[ANY] * 2, out_specs=VMEM, out_shape...  3.49 us
    pallas_call x1, Pallas kernels, middle(): pl.pallas_call(middle_kernel, in_specs=[VMEM], out_specs=[VMEM] * 2, out_...  2.28 us
  transfers between devices with their start and end apart: 2, of which 1 were waited for; matrix products, arithmetic and copies ran while one was open for 0% of the time, Pallas kernels for 2%

commit v1 on v0

--- a/solution.py
+++ b/solution.py
@@ -78,29 +78,33 @@
     lax.fori_loop(0, chips, start, 0, unroll=8)
     fill_order(early, late)
     index_copy.wait()
-    value = index[...]
-    upper = value.astype(BF16)
-    lower = (value - upper.astype(F32)).astype(BF16)
-    pieces = []
-    for part in (upper, lower):
+    rest = index[...]
+    value = jnp.zeros((count, USED), F32)
+    for _ in range(3):
+        part = rest.astype(BF16)
+        rest = rest - part.astype(F32)
         first = lax.dot_general(
             early[...], part[:, :ahead], (((1,), (1,)), ((), ())), preferred_element_type=F32
         )
         second = lax.dot_general(
             late[...], part[:, ahead:], (((1,), (1,)), ((), ())), preferred_element_type=F32
         )
-        for r in range(PHASES):
-            pieces.append(
+        later = count - EARLY
+        value = value + jnp.concatenate(
+            [
                 jnp.concatenate(
-                    [
-                        first[r * EARLY : (r + 1) * EARLY],
-                        second[r * (count - EARLY) : (r + 1) * (count - EARLY)],
-                    ],
-                    0,
+                    [first[r * EARLY : (r + 1) * EARLY], second[r * later : (r + 1) * later]], 0
                 )
-            )
-        pieces.append(jnp.zeros((count, HALF - USED), F32))
-    rows = jnp.concatenate(pieces, axis=1).astype(BF16)
+                for r in range(PHASES)
+            ],
+            1,
+        )
+    origin = value[0:1].astype(BF16).astype(F32)
+    top = lax.broadcasted_iota(jnp.int32, value.shape, 0) == 0
+    value = jnp.where(top, value, value - origin)
+    upper = value.astype(BF16).astype(F32)
+    blank = jnp.zeros((count, HALF - USED), F32)
+    rows = jnp.concatenate([upper, blank, value - upper, blank], 1).astype(BF16)
 
     def repeat(place, _):
         sent_ref[place, t_dev:, :] = rows
@@ -132,7 +136,12 @@
 
 def joined(raw):
     wide = raw.astype(F32)
-    return wide + pltpu.roll(wide, HALF, 1)
+    turned = pltpu.roll(wide, HALF, 1)
+    value = wide + turned
+    lane = lax.broadcasted_iota(jnp.int32, (1, LANES), 1)
+    origin = jnp.where(lane < HALF, wide[0:1], turned[0:1])
+    top = lax.broadcasted_iota(jnp.int32, value.shape, 0) == 0
+    return jnp.where(top, value, value + origin)
 
 
 def summed(value):
@@ -216,7 +225,7 @@
 def spread_kernel(
     own, mine_ref, other_ref, square_ref, days,
     kept_ref, passed_ref, stat_ref,
-    edge, line, slid, win, acc, merged,
+    edge, line, slid, win, late_win, acc, merged,
 ):
     chips, count, _ = own.shape
     core = lax.rem(lax.axis_index(TM), CORES)
@@ -247,37 +256,62 @@
 
     lax.fori_loop(0, chips, move, 0, unroll=16)
 
-    def slide(group, sums):
+    def slide(group, sums, target, offset, base):
         sums = list(sums)
         for side in range(8):
             place = 8 * group + side
             chip = chip_at(place)
-            line[side, 0:8, :] = centered(edge[chip + core, 8:16, :])
-            line[side, 8 : 8 + count, :] = jnp.where(lane == USED, 1.0, centered(own[place]))
-            line[side, 8 + count :, :] = centered(edge[chip + core + 1, 0:8, :])
+            at = base + side
+            line[at, 0:8, :] = centered(edge[chip + core, 8:16, :])
+            line[at, 8 : 8 + count, :] = jnp.where(lane == USED, 1.0, centered(own[place]))
+            line[at, 8 + count :, :] = centered(edge[chip + core + 1, 0:8, :])
+            sums[0] = sums[0] + line[at, 0:16, :] - line[at, count : count + 16, :]
+            sums[1] = sums[1] + summed(line[at, 8 : 8 + count, :])
         for side in range(8):
-            slid[side, 0 : count + 15, :] = jnp.where(
-                lane < HALF, line[side, 0 : count + 15, :], line[side, 1 : count + 16, :]
+            at = base + side
+            slid[at, 0 : count + 15, :] = jnp.where(
+                lane < HALF, line[at, 0 : count + 15, :], line[at, 1 : count + 16, :]
             )
-        start = pl.multiple_of(group * 8 * count, 16)
-        for pair in range(4):
+        start = (8 * group - offset) * count
+        if not isinstance(start, int):
+            start = pl.multiple_of(start, 16)
+        for pair in range(8 // 2):
             for q in range(TILES):
                 tile = jnp.concatenate(
-                    [slid[2 * pair + side, 2 * q : 2 * q + count, :] for side in range(2)], 0
+                    [slid[base + 2 * pair + side, 2 * q : 2 * q + count, :] for side in range(2)], 0
                 )
-                sums[q] = sums[q] + summed(tile)
-                win[q, pl.ds(start + pair * 2 * count, 2 * count), :] = tile.astype(BF16)
+                target[q, pl.ds(start + pair * 2 * count, 2 * count), :] = tile.astype(BF16)
         return tuple(sums)
 
-    window_sums = lax.fori_loop(0, chips // 8, slide, (zero,) * TILES)
-    acc[0:WIDTH, :] = lax.dot_general(
-        jnp.concatenate([win[q] for q in range(TILES)], 1),
-        jnp.concatenate([days[r] for r in range(PHASES)], 1),
-        (((0,), (0,)), ((), ())),
-        preferred_element_type=F32,
-    )
+    def multiply(source, rows):
+        return lax.dot_general(
+            jnp.concatenate([source[q] for q in range(TILES)], 1),
+            jnp.concatenate([days[r, rows, :] for r in range(PHASES)], 1),
+            (((0,), (0,)), ((), ())),
+            preferred_element_type=F32,
+        )
+
+    half = chips // 2
+    window_sums = lax.fori_loop(
+        0, half // 8, lambda g, sums: slide(g, sums, win, 0, 0), (jnp.zeros((16, LANES), F32), zero)
+    )
+    acc[0:WIDTH, :] = multiply(win, slice(0, half * count))
+    for group in range(half // 8, chips // 8):
+        window_sums = slide(group, window_sums, late_win, half, 8 * (group % 2))
+    acc[0:WIDTH, :] += multiply(late_win, slice(half * count, chips * count))
+    edges, inner = window_sums
     acc[WIDTH:, :] = jnp.zeros((HALF, PHASES * LANES), F32)
-    sums_row = jnp.concatenate([jnp.sum(s, 0, keepdims=True) for s in window_sums], 1)
+    inner = jnp.sum(inner, 0, keepdims=True)
+    at = lax.broadcasted_iota(jnp.int32, (16, LANES), 0)
+    upper_half = (lax.broadcasted_iota(jnp.int32, (16, LANES), 1) >= HALF).astype(jnp.int32)
+    window_sums = []
+    for q in range(TILES):
+        move = 2 * q - BEFORE + upper_half
+        gained = (at >= 8 + move) & (at < 8)
+        lost = (at >= 8) & (at < 8 + move)
+        change = jnp.where(gained, edges, 0.0) - jnp.where(lost, edges, 0.0)
+        window_sums.append(inner + jnp.sum(change, 0, keepdims=True))
+    sums_row = jnp.concatenate(window_sums, 1)
 
     def shifted(parts):
         total = parts[0]
@@ -329,9 +363,10 @@
         ],
         scratch_shapes=[
             pltpu.VMEM((chips + 2, 16, LANES), F32),
-            pltpu.VMEM((8, count + 16, LANES), F32),
-            pltpu.VMEM((8, count + 16, LANES), F32),
-            pltpu.VMEM((TILES, chips * count, LANES), BF16),
+            pltpu.VMEM((16, count + 16, LANES), F32),
+            pltpu.VMEM((16, count + 16, LANES), F32),
+            pltpu.VMEM((TILES, chips * count // 2, LANES), BF16),
+            pltpu.VMEM((TILES, chips * count // 2, LANES), BF16),
             pltpu.VMEM((WIDTH + HALF, PHASES * LANES), F32),
             pltpu.VMEM((LANES, WIDTH), F32),
         ],

time: 103 us -> 103 us (level)
  no operation moved by 1% of the time
where the time goes in v1:
time: 103 us
  blocking collectives  84 us (82%)
  Pallas kernels  14.9 us (14%)
  starting transfers between devices  1.95 us (2%)
  waiting for transfers between devices  1.56 us (2%)
    all_to_all x1, blocking collectives, shards(): lax.all_to_all(pack(field, index), TM, 0, 0, axis_index_groups=groups, ti...  84 us
    pallas_call x1, Pallas kernels, spread(): pl.pallas_call(spread_kernel, in_specs=[VMEM] * 5, out_specs=[VMEM] * 3,...  6.76 us
    pallas_call x1, Pallas kernels, pack(): pl.pallas_call(pack_kernel, in_specs=[ANY] * 2, out_specs=VMEM, out_shape...  3.49 us
    pallas_call x1, Pallas kernels, middle(): pl.pallas_call(middle_kernel, in_specs=[VMEM], out_specs=[VMEM] * 2, out_...  2.28 us
  transfers between devices with their start and end apart: 2, of which 1 were waited for; matrix products, arithmetic and copies ran while one was open for 0% of the time, Pallas kernels for 2%

profile of v1, /device:TPU:1, one launch (start us, length us, event | category | flops | bytes accessed | tf_op | source)
XLA Modules:
  0.0 102.5 jit_solution(17656388121487005108)
XLA Ops:
  0.0 3.5 %shard_map.55 = bf16[64,392,128]{2,1,0:T(8,128)(2,1)S(1)} custom-call(bf16[336,8192]{1,0:T(8,128)(2,1)} %field_ref.1, f32[10,336]{1,0:T(8,128)} %bitcast.8), custom_call_target="tpu_custom_call" | custom-call | tf_op jit(solution)/shard_map/pallas_call | solution.py:125
  3.5 84.0 %all_to_all.5.got_ref = bf16[64,392,128]{2,1,0:T(8,128)(2,1)S(1)} all-to-all(bf16[64,392,128]{2,1,0:T(8,128)(2,1)S(1)} %shard_map.55), channel_id=1, replica_groups={{118,126,102,110,86,94,70,78,54,62,38,46,22,30,6,14,116,124,100,108,84,..., dimensions={0} | all-to-all | bytes 12845056 | tf_op jit(solution)/shard_map/all_to_all | solution.py:462
  87.5 0.7 shard_map.56
  88.2 1.9 %collective-permute-start = (f32[65,16,128]{2,1,0:T(8,128)S(1)}, f32[65,16,128]{2,1,0:T(8,128)S(1)}, u32[]{:S(2)}, u32[]{:S(2)}) collective-permute-start(f32[65,16,128]{2,1,0:T(8,128)S(1)} %get-tuple-element.13.mine_ref), channel_id=1, source_target_pairs={{0,1},{1,0},{2,3},{3,2},{4,5},{5,4},{6,7},{7,6},{8,9},{9,8},{10,11... | collective-permute-start | bytes 1597448 | tf_op jit(solution)/shard_map/ppermute | solution.py:468
  90.1 2.3 %shard_map.57 = (bf16[6,3584,128]{2,1,0:T(8,128)(2,1)S(1)}, f32[16,128]{1,0:T(8,128)S(1)}) custom-call(bf16[64,392,128]{2,1,0:T(8,128)(2,1)S(1)} %all_to_all.5.got_ref), custom_call_target="tpu_custom_call" | custom-call | tf_op jit(solution)/shard_map/pallas_call | solution.py:212
  92.4 0.0 copy-start
  92.4 0.0 copy-start.1
  92.4 0.0 copy-start.2
  92.4 0.0 collective-permute-done.other_ref
  92.4 6.8 %shard_map.58 = (f32[80,896]{1,0:T(8,128)S(1)}, f32[80,896]{1,0:T(8,128)S(1)}, f32[8,128]{1,0:T(8,128)S(1)}) custom-call(f32[64,56,128]{2,1,0:T(8,128)S(1)} %get-tuple-element.12.own, f32[65,16,128]{2,1,0:T(8,128)S(1)} %get-tuple-element.13.mine_ref, f32[65,16,128]{2,1,0:T(8,128)S(1)} %collective-permute-done.other_ref, ...), custom_call_target="tpu_custom_call" | custom-call | tf_op jit(solution)/shard_map/pallas_call | solution.py:355
  99.2 0.1 collective-permute-start.1
  99.3 1.6 %collective-permute-done.1.refs_1_ = f32[80,896]{1,0:T(8,128)S(1)} collective-permute-done((f32[80,896]{1,0:T(8,128)S(1)}, f32[80,896]{1,0:T(8,128)S(1)}, u32[]{:S(2)}, u32[]{:S(2)}) %collective-permute-start.1) | collective-permute-done | bytes 286752 | tf_op jit(solution)/shard_map/ppermute | solution.py:468
  100.8 0.0 copy-done
  100.8 0.0 copy-done.1
  100.8 0.0 copy-done.2
  100.8 1.7 %shard_map.59 = f32[10,64,61]{2,1,0:T(8,128)} custom-call(f32[80,896]{1,0:T(8,128)S(1)} %get-tuple-element.16.refs_0_, f32[80,896]{1,0:T(8,128)S(1)} %collective-permute-done.1.refs_1_, f32[8,128]{1,0:T(8,128)S(1)} %get-tuple-element.18.refs_2_, s32[1,61]{1,0:T(1,128)S(1)} %bitcast.5, s32[1,64]{1,0:T(1,128)S(1)} %bitcast.6, s32[1,10]{1,0:T(1,128)S(1)} %bitcast.7), custom_call_target="tpu_custom_call" | custom-call | tf_op jit(solution)/shard_map/pallas_call | solution.py:428
Async XLA Ops:
  88.2 4.2 %collective-permute-start = (f32[65,16,128]{2,1,0:T(8,128)S(1)}, f32[65,16,128]{2,1,0:T(8,128)S(1)}, u32[]{:S(2)}, u32[]{:S(2)}) collective-permute-start(f32[65,16,128]{2,1,0:T(8,128)S(1)} %get-tuple-element.13.mine_ref), channel_id=1, source_target_pairs={{0,1},{1,0},{2,3},{3,2},{4,5},{5,4},{6,7},{7,6},{8,9},{9,8},{10,11... | collective-permute-start | bytes 1597448 | tf_op jit(solution)/shard_map/ppermute | solution.py:468
  92.4 8.5 %copy-start = (s32[61]{0:T(128)S(1)}, s32[61]{0:T(128)}, u32[]{:S(2)}) copy-start(s32[61]{0:T(128)} %param.7) | copy-start | bytes 736
  92.4 8.5 %copy-start.1 = (s32[64]{0:T(128)S(1)}, s32[64]{0:T(128)}, u32[]{:S(2)}) copy-start(s32[64]{0:T(128)} %param.9) | copy-start | bytes 772
  92.4 8.4 %copy-start.2 = (s32[10]{0:T(128)S(1)}, s32[10]{0:T(128)}, u32[]{:S(2)}) copy-start(s32[10]{0:T(128)} %param.8) | copy-start | bytes 124
  99.2 1.7 %collective-permute-start.1 = (f32[80,896]{1,0:T(8,128)S(1)}, f32[80,896]{1,0:T(8,128)S(1)}, u32[]{:S(2)}, u32[]{:S(2)}) collective-permute-start(f32[80,896]{1,0:T(8,128)S(1)} %get-tuple-element.17), channel_id=1, source_target_pairs={{0,1},{1,0},{2,3},{3,2},{4,5},{5,4},{6,7},{7,6},{8,9},{9,8},{10,11... | collective-permute-start | bytes 860168 | tf_op jit(solution)/shard_map/ppermute | solution.py:468

commit v2 on v1

--- a/solution.py
+++ b/solution.py
@@ -161,7 +161,7 @@
         edge_ref[chip, 8:16, :] = value[count - 8 :]
         return first + summed(value), second + summed(value * value)
 
-    first, second = lax.fori_loop(0, chips, body, (zero, zero), unroll=16)
+    first, second = lax.fori_loop(0, chips, body, (zero, zero), unroll=32)
     edge_ref[chips, 0:8, :] = first
     edge_ref[chips, 8:16, :] = second
 
@@ -204,7 +204,7 @@
                 days_ref[r, pl.ds(start + count + base, length), :] = piece[:, LANES:]
         return square
 
-    square_ref[...] = lax.fori_loop(0, chips // 2, body, jnp.zeros((16, LANES), F32), unroll=8)
+    square_ref[...] = lax.fori_loop(0, chips // 2, body, jnp.zeros((16, LANES), F32), unroll=16)
 
 
 def middle(got, t_dev):

time: 103 us -> 102 us (level)
  no operation moved by 1% of the time
where the time goes in v2:
time: 102 us
  blocking collectives  84 us (82%)
  Pallas kernels  14.5 us (14%)
  starting transfers between devices  1.95 us (2%)
  waiting for transfers between devices  1.56 us (2%)
    all_to_all x1, blocking collectives, shards(): lax.all_to_all(pack(field, index), TM, 0, 0, axis_index_groups=groups, ti...  84 us
    pallas_call x1, Pallas kernels, spread(): pl.pallas_call(spread_kernel, in_specs=[VMEM] * 5, out_specs=[VMEM] * 3,...  6.76 us
    pallas_call x1, Pallas kernels, pack(): pl.pallas_call(pack_kernel, in_specs=[ANY] * 2, out_specs=VMEM, out_shape...  3.49 us
  transfers between devices with their start and end apart: 2, of which 1 were waited for; matrix products, arithmetic and copies ran while one was open for 0% of the time, Pallas kernels for 2%

profile of v2, /device:TPU:1, one launch (start us, length us, event | category | flops | bytes accessed | tf_op | source)
XLA Modules:
  0.0 102.1 jit_solution(7477644010827510862)
XLA Ops:
  0.0 3.5 %shard_map.55 = bf16[64,392,128]{2,1,0:T(8,128)(2,1)S(1)} custom-call(bf16[336,8192]{1,0:T(8,128)(2,1)} %field_ref.1, f32[10,336]{1,0:T(8,128)} %bitcast.8), custom_call_target="tpu_custom_call" | custom-call | tf_op jit(solution)/shard_map/pallas_call | solution.py:125
  3.5 84.0 %all_to_all.5.got_ref = bf16[64,392,128]{2,1,0:T(8,128)(2,1)S(1)} all-to-all(bf16[64,392,128]{2,1,0:T(8,128)(2,1)S(1)} %shard_map.55), channel_id=1, replica_groups={{118,126,102,110,86,94,70,78,54,62,38,46,22,30,6,14,116,124,100,108,84,..., dimensions={0} | all-to-all | bytes 12845056 | tf_op jit(solution)/shard_map/all_to_all | solution.py:462
  87.5 0.6 shard_map.56
  88.1 1.9 %collective-permute-start = (f32[65,16,128]{2,1,0:T(8,128)S(1)}, f32[65,16,128]{2,1,0:T(8,128)S(1)}, u32[]{:S(2)}, u32[]{:S(2)}) collective-permute-start(f32[65,16,128]{2,1,0:T(8,128)S(1)} %get-tuple-element.13.mine_ref), channel_id=1, source_target_pairs={{0,1},{1,0},{2,3},{3,2},{4,5},{5,4},{6,7},{7,6},{8,9},{9,8},{10,11... | collective-permute-start | bytes 1597448 | tf_op jit(solution)/shard_map/ppermute | solution.py:468
  90.0 2.0 %shard_map.57 = (bf16[6,3584,128]{2,1,0:T(8,128)(2,1)S(1)}, f32[16,128]{1,0:T(8,128)S(1)}) custom-call(bf16[64,392,128]{2,1,0:T(8,128)(2,1)S(1)} %all_to_all.5.got_ref), custom_call_target="tpu_custom_call" | custom-call | tf_op jit(solution)/shard_map/pallas_call | solution.py:212
  91.9 0.0 copy-start
  92.0 0.0 copy-start.1
  92.0 0.0 copy-start.2
  92.0 0.0 collective-permute-done.other_ref
  92.0 6.8 %shard_map.58 = (f32[80,896]{1,0:T(8,128)S(1)}, f32[80,896]{1,0:T(8,128)S(1)}, f32[8,128]{1,0:T(8,128)S(1)}) custom-call(f32[64,56,128]{2,1,0:T(8,128)S(1)} %get-tuple-element.12.own, f32[65,16,128]{2,1,0:T(8,128)S(1)} %get-tuple-element.13.mine_ref, f32[65,16,128]{2,1,0:T(8,128)S(1)} %collective-permute-done.other_ref, ...), custom_call_target="tpu_custom_call" | custom-call | tf_op jit(solution)/shard_map/pallas_call | solution.py:355
  98.8 0.1 collective-permute-start.1
  98.8 1.6 %collective-permute-done.1.refs_1_ = f32[80,896]{1,0:T(8,128)S(1)} collective-permute-done((f32[80,896]{1,0:T(8,128)S(1)}, f32[80,896]{1,0:T(8,128)S(1)}, u32[]{:S(2)}, u32[]{:S(2)}) %collective-permute-start.1) | collective-permute-done | bytes 286752 | tf_op jit(solution)/shard_map/ppermute | solution.py:468
  100.4 0.0 copy-done
  100.4 0.0 copy-done.1
  100.4 0.0 copy-done.2
  100.4 1.7 %shard_map.59 = f32[10,64,61]{2,1,0:T(8,128)} custom-call(f32[80,896]{1,0:T(8,128)S(1)} %get-tuple-element.16.refs_0_, f32[80,896]{1,0:T(8,128)S(1)} %collective-permute-done.1.refs_1_, f32[8,128]{1,0:T(8,128)S(1)} %get-tuple-element.18.refs_2_, s32[1,61]{1,0:T(1,128)S(1)} %bitcast.5, s32[1,64]{1,0:T(1,128)S(1)} %bitcast.6, s32[1,10]{1,0:T(1,128)S(1)} %bitcast.7), custom_call_target="tpu_custom_call" | custom-call | tf_op jit(solution)/shard_map/pallas_call | solution.py:428
Async XLA Ops:
  88.1 3.9 %collective-permute-start = (f32[65,16,128]{2,1,0:T(8,128)S(1)}, f32[65,16,128]{2,1,0:T(8,128)S(1)}, u32[]{:S(2)}, u32[]{:S(2)}) collective-permute-start(f32[65,16,128]{2,1,0:T(8,128)S(1)} %get-tuple-element.13.mine_ref), channel_id=1, source_target_pairs={{0,1},{1,0},{2,3},{3,2},{4,5},{5,4},{6,7},{7,6},{8,9},{9,8},{10,11... | collective-permute-start | bytes 1597448 | tf_op jit(solution)/shard_map/ppermute | solution.py:468
  91.9 8.5 %copy-start = (s32[61]{0:T(128)S(1)}, s32[61]{0:T(128)}, u32[]{:S(2)}) copy-start(s32[61]{0:T(128)} %param.7) | copy-start | bytes 736
  92.0 8.5 %copy-start.1 = (s32[64]{0:T(128)S(1)}, s32[64]{0:T(128)}, u32[]{:S(2)}) copy-start(s32[64]{0:T(128)} %param.9) | copy-start | bytes 772
  92.0 8.4 %copy-start.2 = (s32[10]{0:T(128)S(1)}, s32[10]{0:T(128)}, u32[]{:S(2)}) copy-start(s32[10]{0:T(128)} %param.8) | copy-start | bytes 124
  98.8 1.7 %collective-permute-start.1 = (f32[80,896]{1,0:T(8,128)S(1)}, f32[80,896]{1,0:T(8,128)S(1)}, u32[]{:S(2)}, u32[]{:S(2)}) collective-permute-start(f32[80,896]{1,0:T(8,128)S(1)} %get-tuple-element.17), channel_id=1, source_target_pairs={{0,1},{1,0},{2,3},{3,2},{4,5},{5,4},{6,7},{7,6},{8,9},{9,8},{10,11... | collective-permute-start | bytes 860168 | tf_op jit(solution)/shard_map/ppermute | solution.py:468

commit v3 on v2

--- a/solution.py
+++ b/solution.py
@@ -79,6 +79,21 @@
     fill_order(early, late)
     index_copy.wait()
     rest = index[...]
+    gap = jnp.zeros((16 - kcount, 1), F32)
+    rest_sums = jnp.concatenate(
+        [
+            jnp.sum(rest, 1, keepdims=True),
+            gap,
+            jnp.sum(rest * rest, 1, keepdims=True),
+            jnp.zeros((count - 16 - kcount, 1), F32),
+        ],
+        0,
+    )
+    spare = []
+    for _ in range(3):
+        spare.append(rest_sums.astype(BF16).astype(F32))
+        rest_sums = rest_sums - spare[-1]
+    spare.append(jnp.zeros((count, 1), F32))
     value = jnp.zeros((count, USED), F32)
     for _ in range(3):
         part = rest.astype(BF16)
@@ -104,7 +119,7 @@
     value = jnp.where(top, value, value - origin)
     upper = value.astype(BF16).astype(F32)
     blank = jnp.zeros((count, HALF - USED), F32)
-    rows = jnp.concatenate([upper, blank, value - upper, blank], 1).astype(BF16)
+    rows = jnp.concatenate([upper] + spare + [value - upper, blank], 1).astype(BF16)
 
     def repeat(place, _):
         sent_ref[place, t_dev:, :] = rows
@@ -148,34 +163,36 @@
     return jnp.sum(value.reshape(-1, 8, LANES), 0)
 
 
-def take_kernel(got_ref, own_ref, edge_ref):
-    chips, count, _ = own_ref.shape
-    zero = jnp.zeros((8, LANES), F32)
+def take_kernel(got_ref, edge_ref):
+    chips, rows, _ = got_ref.shape
+    count = rows // (PHASES + 1)
+    start = rows - count
+    lane = lax.broadcasted_iota(jnp.int32, (1, LANES), 1)
+    top = lax.broadcasted_iota(jnp.int32, (8, LANES), 0) == 0
 
     def body(place, sums):
-        first, second = sums
+        head = got_ref[place, start : start + 32, :].astype(F32)
+        tail = got_ref[place, rows - 8 :, :].astype(F32)
+        turned = pltpu.roll(head[0:8], HALF, 1)
+        origin = jnp.where(lane < HALF, head[0:1], turned[0:1])
+        value = head[0:8] + turned
         chip = chip_at(place)
-        value = joined(got_ref[place, PHASES * count :, :])
-        own_ref[place] = value
-        edge_ref[chip, 0:8, :] = value[0:8]
-        edge_ref[chip, 8:16, :] = value[count - 8 :]
-        return first + summed(value), second + summed(value * value)
-
-    first, second = lax.fori_loop(0, chips, body, (zero, zero), unroll=32)
-    edge_ref[chips, 0:8, :] = first
-    edge_ref[chips, 8:16, :] = second
-
-
-def take_index(got, count):
-    chips = got.shape[0]
+        edge_ref[chip, 0:8, :] = jnp.where(top, value, value + origin)
+        edge_ref[chip, 8:16, :] = tail + pltpu.roll(tail, HALF, 1) + origin
+        return sums + head
+
+    sums = lax.fori_loop(0, chips, body, jnp.zeros((32, LANES), F32), unroll=64)
+    spare = (lane >= USED) & (lane < HALF)
+    sums = jnp.sum(jnp.where(spare, sums, 0.0), 1, keepdims=True)
+    edge_ref[chips] = jnp.where(lane == 0, sums[0:16], jnp.where(lane == 1, sums[16:32], 0.0))
+
+
+def take_index(got):
     return pl.pallas_call(
         take_kernel,
         in_specs=[VMEM],
-        out_specs=[VMEM] * 2,
-        out_shape=[
-            pltpu.VMEM((chips, count, LANES), F32),
-            pltpu.VMEM((chips + 1, 16, LANES), F32),
-        ],
+        out_specs=VMEM,
+        out_shape=pltpu.VMEM((got.shape[0] + 1, 16, LANES), F32),
         compiler_params=SMALL,
     )(local(got))
 
@@ -204,7 +221,7 @@
                 days_ref[r, pl.ds(start + count + base, length), :] = piece[:, LANES:]
         return square
 
-    square_ref[...] = lax.fori_loop(0, chips // 2, body, jnp.zeros((16, LANES), F32), unroll=16)
+    square_ref[...] = lax.fori_loop(0, chips // 2, body, jnp.zeros((16, LANES), F32), unroll=32)
 
 
 def middle(got, t_dev):
@@ -223,23 +240,23 @@
 
 
 def spread_kernel(
-    own, mine_ref, other_ref, square_ref, days,
+    got_ref, mine_ref, other_ref, square_ref, days,
     kept_ref, passed_ref, stat_ref,
     edge, line, slid, win, late_win, acc, merged,
 ):
-    chips, count, _ = own.shape
+    chips, rows, _ = got_ref.shape
+    count = rows // (PHASES + 1)
     core = lax.rem(lax.axis_index(TM), CORES)
     total_days = 2.0 * chips * count * PHASES
     zero = jnp.zeros((8, LANES), F32)
     sums = mine_ref[chips] + other_ref[chips]
-    row = lax.broadcasted_iota(jnp.int32, (LANES, LANES), 0)
-    column = lax.broadcasted_iota(jnp.int32, (LANES, LANES), 1) % HALF
-    same = (row < USED) & (column < USED) & (row % KCOUNT == column % KCOUNT)
-    folded = jnp.dot(
-        sums, same.astype(F32), precision=lax.Precision.HIGHEST, preferred_element_type=F32
-    )
-    mean = jnp.sum(folded[0:8], 0, keepdims=True) / total_days
-    var = jnp.sum(folded[8:16], 0, keepdims=True) / total_days - mean * mean
+    mean = sums[:, 0:1] / total_days
+    var = sums[:, 1:2] / total_days - mean * mean
+    row = lax.broadcasted_iota(jnp.int32, (16, LANES), 0)
+    column = lax.broadcasted_iota(jnp.int32, (16, LANES), 1) % HALF
+    same = (column < USED) & (column % KCOUNT == row)
+    mean = jnp.sum(jnp.where(same, mean, 0.0), 0, keepdims=True)
+    var = jnp.sum(jnp.where(same, var, 0.0), 0, keepdims=True)
     stat_ref[...] = jnp.concatenate([mean, var, jnp.zeros((6, LANES), F32)], 0)
     lane = lax.broadcasted_iota(jnp.int32, (1, LANES), 1)
     valid = lane % HALF < USED
@@ -263,7 +280,7 @@
             chip = chip_at(place)
             at = base + side
             line[at, 0:8, :] = centered(edge[chip + core, 8:16, :])
-            line[at, 8 : 8 + count, :] = jnp.where(lane == USED, 1.0, centered(own[place]))
+            line[at, 8 : 8 + count, :] = jnp.where(lane == USED, 1.0, centered(joined(got_ref[place, rows - count :, :])))
             line[at, 8 + count :, :] = centered(edge[chip + core + 1, 0:8, :])
             sums[0] = sums[0] + line[at, 0:16, :] - line[at, count : count + 16, :]
             sums[1] = sums[1] + summed(line[at, 8 : 8 + count, :])
@@ -293,7 +310,8 @@
 
     half = chips // 2
     window_sums = lax.fori_loop(
-        0, half // 8, lambda g, sums: slide(g, sums, win, 0, 0), (jnp.zeros((16, LANES), F32), zero)
+        0, half // 8, lambda g, sums: slide(g, sums, win, 0, 0), (jnp.zeros((16, LANES), F32), zero),
+        unroll=True,
     )
     acc[0:WIDTH, :] = multiply(win, slice(0, half * count))
     for group in range(half // 8, chips // 8):
@@ -350,8 +368,9 @@
         target[HALF + 8 :, :] = totals
 
 
-def spread(own, mine, other, square, days):
-    chips, count, _ = own.shape
+def spread(got, mine, other, square, days):
+    chips, rows, _ = got.shape
+    count = rows // (PHASES + 1)
     return pl.pallas_call(
         spread_kernel,
         in_specs=[VMEM] * 5,
@@ -371,7 +390,7 @@
             pltpu.VMEM((LANES, WIDTH), F32),
         ],
         compiler_params=pltpu.CompilerParams(vmem_limit_bytes=32 << 20),
-    )(local(own), local(mine), local(other), local(square), local(days))
+    )(local(got), local(mine), local(other), local(square), local(days))
 
 
 def finish_kernel(
@@ -444,10 +463,10 @@
 
 def after(got, lag_list, index_offset, sea_mask, total_days, swapped):
     t_dev = got.shape[1] * PHASES // (PHASES + 1)
-    own, mine = take_index(got, t_dev // PHASES)
+    mine = take_index(got)
     other = swapped(mine)
     days, square = middle(got, t_dev)
-    kept, passed, stat = spread(own, mine, other, square, days)
+    kept, passed, stat = spread(got, mine, other, square, days)
     taken = swapped(passed)
     maps = finish(kept, taken, stat, lag_list, index_offset, sea_mask, total_days)
     return jnp.transpose(maps, (1, 0, 2))

time: 102 us -> 101 us (level)
  Pallas kernels: 14.5 us -> 13.4 us
where the time goes in v3:
time: 101 us
  blocking collectives  84 us (83%)
  Pallas kernels  13.4 us (13%)
  starting transfers between devices  2.12 us (2%)
  waiting for transfers between devices  1.4 us (1%)
    all_to_all x1, blocking collectives, shards(): lax.all_to_all(pack(field, index), TM, 0, 0, axis_index_groups=groups, ti...  84 us
    pallas_call x1, Pallas kernels, spread(): pl.pallas_call(spread_kernel, in_specs=[VMEM] * 5, out_specs=[VMEM] * 3,...  6.35 us
    pallas_call x1, Pallas kernels, pack(): pl.pallas_call(pack_kernel, in_specs=[ANY] * 2, out_specs=VMEM, out_shape...  3.49 us
    ppermute x2, starting transfers between devices, shards(): lax.ppermute(x, TM, swap)  2.12 us
  transfers between devices with their start and end apart: 2, of which 1 were waited for; matrix products, arithmetic and copies ran while one was open for 0% of the time, Pallas kernels for 2%

profile of v3, /device:TPU:1, one launch (start us, length us, event | category | flops | bytes accessed | tf_op | source)
XLA Modules:
  0.0 101.0 jit_solution(5267145833964260699)
XLA Ops:
  0.0 3.5 %shard_map.55 = bf16[64,392,128]{2,1,0:T(8,128)(2,1)S(1)} custom-call(bf16[336,8192]{1,0:T(8,128)(2,1)} %field_ref.1, f32[10,336]{1,0:T(8,128)} %bitcast.8), custom_call_target="tpu_custom_call" | custom-call | tf_op jit(solution)/shard_map/pallas_call | solution.py:140
  3.5 84.0 %all_to_all.5.got_ref = bf16[64,392,128]{2,1,0:T(8,128)(2,1)S(1)} all-to-all(bf16[64,392,128]{2,1,0:T(8,128)(2,1)S(1)} %shard_map.55), channel_id=1, replica_groups={{118,126,102,110,86,94,70,78,54,62,38,46,22,30,6,14,116,124,100,108,84,..., dimensions={0} | all-to-all | bytes 12845056 | tf_op jit(solution)/shard_map/all_to_all | solution.py:481
  87.5 0.2 shard_map.56.mine_ref
  87.7 1.9 %collective-permute-start = (f32[65,16,128]{2,1,0:T(8,128)S(1)}, f32[65,16,128]{2,1,0:T(8,128)S(1)}, u32[]{:S(2)}, u32[]{:S(2)}) collective-permute-start(f32[65,16,128]{2,1,0:T(8,128)S(1)} %shard_map.56.mine_ref), channel_id=1, source_target_pairs={{0,1},{1,0},{2,3},{3,2},{4,5},{5,4},{6,7},{7,6},{8,9},{9,8},{10,11... | collective-permute-start | bytes 1597448 | tf_op jit(solution)/shard_map/ppermute | solution.py:487
  89.6 1.7 %shard_map.57 = (bf16[6,3584,128]{2,1,0:T(8,128)(2,1)S(1)}, f32[16,128]{1,0:T(8,128)S(1)}) custom-call(bf16[64,392,128]{2,1,0:T(8,128)(2,1)S(1)} %all_to_all.5.got_ref), custom_call_target="tpu_custom_call" | custom-call | tf_op jit(solution)/shard_map/pallas_call | solution.py:229
  91.3 0.0 collective-permute-done.other_ref
  91.3 0.0 copy-start
  91.3 0.0 copy-start.1
  91.3 0.0 copy-start.2
  91.3 6.3 %shard_map.58 = (f32[80,896]{1,0:T(8,128)S(1)}, f32[80,896]{1,0:T(8,128)S(1)}, f32[8,128]{1,0:T(8,128)S(1)}) custom-call(bf16[64,392,128]{2,1,0:T(8,128)(2,1)S(1)} %all_to_all.5.got_ref, f32[65,16,128]{2,1,0:T(8,128)S(1)} %shard_map.56.mine_ref, f32[65,16,128]{2,1,0:T(8,128)S(1)} %collective-permute-done.other_ref, ...), custom_call_target="tpu_custom_call" | custom-call | tf_op jit(solution)/shard_map/pallas_call | solution.py:374
  97.7 0.3 collective-permute-start.1
  97.9 1.4 %collective-permute-done.1.refs_1_ = f32[80,896]{1,0:T(8,128)S(1)} collective-permute-done((f32[80,896]{1,0:T(8,128)S(1)}, f32[80,896]{1,0:T(8,128)S(1)}, u32[]{:S(2)}, u32[]{:S(2)}) %collective-permute-start.1) | collective-permute-done | bytes 286752 | tf_op jit(solution)/shard_map/ppermute | solution.py:487
  99.3 0.0 copy-done
  99.3 0.0 copy-done.1
  99.3 0.0 copy-done.2
  99.3 1.7 %shard_map.59 = f32[10,64,61]{2,1,0:T(8,128)} custom-call(f32[80,896]{1,0:T(8,128)S(1)} %get-tuple-element.12.refs_0_, f32[80,896]{1,0:T(8,128)S(1)} %collective-permute-done.1.refs_1_, f32[8,128]{1,0:T(8,128)S(1)} %get-tuple-element.14.refs_2_, s32[1,61]{1,0:T(1,128)S(1)} %bitcast.5, s32[1,64]{1,0:T(1,128)S(1)} %bitcast.6, s32[1,10]{1,0:T(1,128)S(1)} %bitcast.7), custom_call_target="tpu_custom_call" | custom-call | tf_op jit(solution)/shard_map/pallas_call | solution.py:447
Async XLA Ops:
  87.7 3.6 %collective-permute-start = (f32[65,16,128]{2,1,0:T(8,128)S(1)}, f32[65,16,128]{2,1,0:T(8,128)S(1)}, u32[]{:S(2)}, u32[]{:S(2)}) collective-permute-start(f32[65,16,128]{2,1,0:T(8,128)S(1)} %shard_map.56.mine_ref), channel_id=1, source_target_pairs={{0,1},{1,0},{2,3},{3,2},{4,5},{5,4},{6,7},{7,6},{8,9},{9,8},{10,11... | collective-permute-start | bytes 1597448 | tf_op jit(solution)/shard_map/ppermute | solution.py:487
  91.3 8.0 %copy-start = (s32[61]{0:T(128)S(1)}, s32[61]{0:T(128)}, u32[]{:S(2)}) copy-start(s32[61]{0:T(128)} %param.7) | copy-start | bytes 736
  91.3 8.0 %copy-start.1 = (s32[64]{0:T(128)S(1)}, s32[64]{0:T(128)}, u32[]{:S(2)}) copy-start(s32[64]{0:T(128)} %param.9) | copy-start | bytes 772
  91.3 8.0 %copy-start.2 = (s32[10]{0:T(128)S(1)}, s32[10]{0:T(128)}, u32[]{:S(2)}) copy-start(s32[10]{0:T(128)} %param.8) | copy-start | bytes 124
  97.7 1.7 %collective-permute-start.1 = (f32[80,896]{1,0:T(8,128)S(1)}, f32[80,896]{1,0:T(8,128)S(1)}, u32[]{:S(2)}, u32[]{:S(2)}) collective-permute-start(f32[80,896]{1,0:T(8,128)S(1)} %get-tuple-element.13), channel_id=1, source_target_pairs={{0,1},{1,0},{2,3},{3,2},{4,5},{5,4},{6,7},{7,6},{8,9},{9,8},{10,11... | collective-permute-start | bytes 860168 | tf_op jit(solution)/shard_map/ppermute | solution.py:487

commit v4 on v3

--- a/solution.py
+++ b/solution.py
@@ -271,7 +271,7 @@
         edge[chip + 1] = other_ref[chip]
         return 0
 
-    lax.fori_loop(0, chips, move, 0, unroll=16)
+    lax.fori_loop(0, chips, move, 0, unroll=64)
 
     def slide(group, sums, target, offset, base):
         sums = list(sums)
@@ -313,9 +313,9 @@
         0, half // 8, lambda g, sums: slide(g, sums, win, 0, 0), (jnp.zeros((16, LANES), F32), zero),
         unroll=True,
     )
-    acc[0:WIDTH, :] = multiply(win, slice(0, half * count))
     for group in range(half // 8, chips // 8):
         window_sums = slide(group, window_sums, late_win, half, 8 * (group % 2))
+    acc[0:WIDTH, :] = multiply(win, slice(0, half * count))
     acc[0:WIDTH, :] += multiply(late_win, slice(half * count, chips * count))
     edges, inner = window_sums
     acc[WIDTH:, :] = jnp.zeros((HALF, PHASES * LANES), F32)

time: 101 us -> 101 us (level)
  no operation moved by 1% of the time
where the time goes in v4:
time: 101 us
  blocking collectives  84 us (83%)
  Pallas kernels  13.3 us (13%)
  starting transfers between devices  2.12 us (2%)
  waiting for transfers between devices  1.4 us (1%)
    all_to_all x1, blocking collectives, shards(): lax.all_to_all(pack(field, index), TM, 0, 0, axis_index_groups=groups, ti...  84 us
    pallas_call x1, Pallas kernels, spread(): pl.pallas_call(spread_kernel, in_specs=[VMEM] * 5, out_specs=[VMEM] * 3,...  6.25 us
    pallas_call x1, Pallas kernels, pack(): pl.pallas_call(pack_kernel, in_specs=[ANY] * 2, out_specs=VMEM, out_shape...  3.49 us
    ppermute x2, starting transfers between devices, shards(): lax.ppermute(x, TM, swap)  2.12 us
  transfers between devices with their start and end apart: 2, of which 1 were waited for; matrix products, arithmetic and copies ran while one was open for 0% of the time, Pallas kernels for 2%

profile of v4, /device:TPU:1, one launch (start us, length us, event | category | flops | bytes accessed | tf_op | source)
XLA Modules:
  0.0 100.9 jit_solution(11660503303971827295)
XLA Ops:
  0.0 3.5 %shard_map.55 = bf16[64,392,128]{2,1,0:T(8,128)(2,1)S(1)} custom-call(bf16[336,8192]{1,0:T(8,128)(2,1)} %field_ref.1, f32[10,336]{1,0:T(8,128)} %bitcast.8), custom_call_target="tpu_custom_call" | custom-call | tf_op jit(solution)/shard_map/pallas_call | solution.py:140
  3.5 84.0 %all_to_all.5.got_ref = bf16[64,392,128]{2,1,0:T(8,128)(2,1)S(1)} all-to-all(bf16[64,392,128]{2,1,0:T(8,128)(2,1)S(1)} %shard_map.55), channel_id=1, replica_groups={{118,126,102,110,86,94,70,78,54,62,38,46,22,30,6,14,116,124,100,108,84,..., dimensions={0} | all-to-all | bytes 12845056 | tf_op jit(solution)/shard_map/all_to_all | solution.py:481
  87.5 0.2 shard_map.56.mine_ref
  87.7 1.9 %collective-permute-start = (f32[65,16,128]{2,1,0:T(8,128)S(1)}, f32[65,16,128]{2,1,0:T(8,128)S(1)}, u32[]{:S(2)}, u32[]{:S(2)}) collective-permute-start(f32[65,16,128]{2,1,0:T(8,128)S(1)} %shard_map.56.mine_ref), channel_id=1, source_target_pairs={{0,1},{1,0},{2,3},{3,2},{4,5},{5,4},{6,7},{7,6},{8,9},{9,8},{10,11... | collective-permute-start | bytes 1597448 | tf_op jit(solution)/shard_map/ppermute | solution.py:487
  89.6 1.7 %shard_map.57 = (bf16[6,3584,128]{2,1,0:T(8,128)(2,1)S(1)}, f32[16,128]{1,0:T(8,128)S(1)}) custom-call(bf16[64,392,128]{2,1,0:T(8,128)(2,1)S(1)} %all_to_all.5.got_ref), custom_call_target="tpu_custom_call" | custom-call | tf_op jit(solution)/shard_map/pallas_call | solution.py:229
  91.3 0.0 collective-permute-done.other_ref
  91.3 0.0 copy-start
  91.3 0.0 copy-start.1
  91.3 0.0 copy-start.2
  91.3 6.2 %shard_map.58 = (f32[80,896]{1,0:T(8,128)S(1)}, f32[80,896]{1,0:T(8,128)S(1)}, f32[8,128]{1,0:T(8,128)S(1)}) custom-call(bf16[64,392,128]{2,1,0:T(8,128)(2,1)S(1)} %all_to_all.5.got_ref, f32[65,16,128]{2,1,0:T(8,128)S(1)} %shard_map.56.mine_ref, f32[65,16,128]{2,1,0:T(8,128)S(1)} %collective-permute-done.other_ref, ...), custom_call_target="tpu_custom_call" | custom-call | tf_op jit(solution)/shard_map/pallas_call | solution.py:374
  97.6 0.2 collective-permute-start.1
  97.8 1.4 %collective-permute-done.1.refs_1_ = f32[80,896]{1,0:T(8,128)S(1)} collective-permute-done((f32[80,896]{1,0:T(8,128)S(1)}, f32[80,896]{1,0:T(8,128)S(1)}, u32[]{:S(2)}, u32[]{:S(2)}) %collective-permute-start.1) | collective-permute-done | bytes 286752 | tf_op jit(solution)/shard_map/ppermute | solution.py:487
  99.2 0.0 copy-done
  99.2 0.0 copy-done.1
  99.2 0.0 copy-done.2
  99.2 1.7 %shard_map.59 = f32[10,64,61]{2,1,0:T(8,128)} custom-call(f32[80,896]{1,0:T(8,128)S(1)} %get-tuple-element.12.refs_0_, f32[80,896]{1,0:T(8,128)S(1)} %collective-permute-done.1.refs_1_, f32[8,128]{1,0:T(8,128)S(1)} %get-tuple-element.14.refs_2_, s32[1,61]{1,0:T(1,128)S(1)} %bitcast.5, s32[1,64]{1,0:T(1,128)S(1)} %bitcast.6, s32[1,10]{1,0:T(1,128)S(1)} %bitcast.7), custom_call_target="tpu_custom_call" | custom-call | tf_op jit(solution)/shard_map/pallas_call | solution.py:447
Async XLA Ops:
  87.7 3.6 %collective-permute-start = (f32[65,16,128]{2,1,0:T(8,128)S(1)}, f32[65,16,128]{2,1,0:T(8,128)S(1)}, u32[]{:S(2)}, u32[]{:S(2)}) collective-permute-start(f32[65,16,128]{2,1,0:T(8,128)S(1)} %shard_map.56.mine_ref), channel_id=1, source_target_pairs={{0,1},{1,0},{2,3},{3,2},{4,5},{5,4},{6,7},{7,6},{8,9},{9,8},{10,11... | collective-permute-start | bytes 1597448 | tf_op jit(solution)/shard_map/ppermute | solution.py:487
  91.3 7.9 %copy-start = (s32[61]{0:T(128)S(1)}, s32[61]{0:T(128)}, u32[]{:S(2)}) copy-start(s32[61]{0:T(128)} %param.7) | copy-start | bytes 736
  91.3 7.9 %copy-start.1 = (s32[64]{0:T(128)S(1)}, s32[64]{0:T(128)}, u32[]{:S(2)}) copy-start(s32[64]{0:T(128)} %param.9) | copy-start | bytes 772
  91.3 7.9 %copy-start.2 = (s32[10]{0:T(128)S(1)}, s32[10]{0:T(128)}, u32[]{:S(2)}) copy-start(s32[10]{0:T(128)} %param.8) | copy-start | bytes 124
  97.6 1.7 %collective-permute-start.1 = (f32[80,896]{1,0:T(8,128)S(1)}, f32[80,896]{1,0:T(8,128)S(1)}, u32[]{:S(2)}, u32[]{:S(2)}) collective-permute-start(f32[80,896]{1,0:T(8,128)S(1)} %get-tuple-element.13), channel_id=1, source_target_pairs={{0,1},{1,0},{2,3},{3,2},{4,5},{5,4},{6,7},{7,6},{8,9},{9,8},{10,11... | collective-permute-start | bytes 860168 | tf_op jit(solution)/shard_map/ppermute | solution.py:487

commit v5 on v4

--- a/solution.py
+++ b/solution.py
@@ -417,12 +417,11 @@
     lag = jnp.concatenate([lag_ref[...], jnp.zeros((1, LANES - lags), jnp.int32)], 1)
     parts = jnp.concatenate([upper, middle, lower], 0)
     copies = []
+    picker = jnp.concatenate([base[16 - k : 16 - k + WIDTH, :].astype(BF16) for k in range(KCOUNT)], 1)
+    thirds = jnp.dot(parts, picker, preferred_element_type=F32)
+    every = thirds[0:ROWS] + thirds[ROWS : 2 * ROWS] + thirds[2 * ROWS :]
     for pair in range(KCOUNT // 2):
-        picker = jnp.concatenate(
-            [base[16 - k : 16 - k + WIDTH, :].astype(BF16) for k in (2 * pair, 2 * pair + 1)], 1
-        )
-        thirds = jnp.dot(parts, picker, preferred_element_type=F32)
-        chosen = thirds[0:ROWS] + thirds[ROWS : 2 * ROWS] + thirds[2 * ROWS :]
+        chosen = every[:, pair * 2 * LANES : (pair + 1) * 2 * LANES]
         for side in range(2):
             k = 2 * pair + side
             part = chosen[:, side * LANES : (side + 1) * LANES]

time: 101 us -> 101 us (level)
  no operation moved by 1% of the time
where the time goes in v5:
time: 101 us
  blocking collectives  84 us (83%)
  Pallas kernels  13.3 us (13%)
  starting transfers between devices  2.12 us (2%)
  waiting for transfers between devices  1.4 us (1%)
    all_to_all x1, blocking collectives, shards(): lax.all_to_all(pack(field, index), TM, 0, 0, axis_index_groups=groups, ti...  84 us
    pallas_call x1, Pallas kernels, spread(): pl.pallas_call(spread_kernel, in_specs=[VMEM] * 5, out_specs=[VMEM] * 3,...  6.25 us
    pallas_call x1, Pallas kernels, pack(): pl.pallas_call(pack_kernel, in_specs=[ANY] * 2, out_specs=VMEM, out_shape...  3.49 us
    ppermute x2, starting transfers between devices, shards(): lax.ppermute(x, TM, swap)  2.12 us
  transfers between devices with their start and end apart: 2, of which 1 were waited for; matrix products, arithmetic and copies ran while one was open for 0% of the time, Pallas kernels for 2%

profile of v5, /device:TPU:1, one launch (start us, length us, event | category | flops | bytes accessed | tf_op | source)
XLA Modules:
  0.0 100.9 jit_solution(10316994786708255598)
XLA Ops:
  0.0 3.5 %shard_map.55 = bf16[64,392,128]{2,1,0:T(8,128)(2,1)S(1)} custom-call(bf16[336,8192]{1,0:T(8,128)(2,1)} %field_ref.1, f32[10,336]{1,0:T(8,128)} %bitcast.8), custom_call_target="tpu_custom_call" | custom-call | tf_op jit(solution)/shard_map/pallas_call | solution.py:140
  3.5 84.0 %all_to_all.5.got_ref = bf16[64,392,128]{2,1,0:T(8,128)(2,1)S(1)} all-to-all(bf16[64,392,128]{2,1,0:T(8,128)(2,1)S(1)} %shard_map.55), channel_id=1, replica_groups={{118,126,102,110,86,94,70,78,54,62,38,46,22,30,6,14,116,124,100,108,84,..., dimensions={0} | all-to-all | bytes 12845056 | tf_op jit(solution)/shard_map/all_to_all | solution.py:480
  87.5 0.2 shard_map.56.mine_ref
  87.7 1.9 %collective-permute-start = (f32[65,16,128]{2,1,0:T(8,128)S(1)}, f32[65,16,128]{2,1,0:T(8,128)S(1)}, u32[]{:S(2)}, u32[]{:S(2)}) collective-permute-start(f32[65,16,128]{2,1,0:T(8,128)S(1)} %shard_map.56.mine_ref), channel_id=1, source_target_pairs={{0,1},{1,0},{2,3},{3,2},{4,5},{5,4},{6,7},{7,6},{8,9},{9,8},{10,11... | collective-permute-start | bytes 1597448 | tf_op jit(solution)/shard_map/ppermute | solution.py:486
  89.6 1.7 %shard_map.57 = (bf16[6,3584,128]{2,1,0:T(8,128)(2,1)S(1)}, f32[16,128]{1,0:T(8,128)S(1)}) custom-call(bf16[64,392,128]{2,1,0:T(8,128)(2,1)S(1)} %all_to_all.5.got_ref), custom_call_target="tpu_custom_call" | custom-call | tf_op jit(solution)/shard_map/pallas_call | solution.py:229
  91.3 0.0 collective-permute-done.other_ref
  91.3 0.0 copy-start
  91.3 0.0 copy-start.1
  91.3 0.0 copy-start.2
  91.3 6.2 %shard_map.58 = (f32[80,896]{1,0:T(8,128)S(1)}, f32[80,896]{1,0:T(8,128)S(1)}, f32[8,128]{1,0:T(8,128)S(1)}) custom-call(bf16[64,392,128]{2,1,0:T(8,128)(2,1)S(1)} %all_to_all.5.got_ref, f32[65,16,128]{2,1,0:T(8,128)S(1)} %shard_map.56.mine_ref, f32[65,16,128]{2,1,0:T(8,128)S(1)} %collective-permute-done.other_ref, ...), custom_call_target="tpu_custom_call" | custom-call | tf_op jit(solution)/shard_map/pallas_call | solution.py:374
  97.6 0.2 collective-permute-start.1
  97.8 1.4 %collective-permute-done.1.refs_1_ = f32[80,896]{1,0:T(8,128)S(1)} collective-permute-done((f32[80,896]{1,0:T(8,128)S(1)}, f32[80,896]{1,0:T(8,128)S(1)}, u32[]{:S(2)}, u32[]{:S(2)}) %collective-permute-start.1) | collective-permute-done | bytes 286752 | tf_op jit(solution)/shard_map/ppermute | solution.py:486
  99.2 0.0 copy-done
  99.2 0.0 copy-done.1
  99.2 0.0 copy-done.2
  99.2 1.7 %shard_map.59 = f32[10,64,61]{2,1,0:T(8,128)} custom-call(f32[80,896]{1,0:T(8,128)S(1)} %get-tuple-element.12.refs_0_, f32[80,896]{1,0:T(8,128)S(1)} %collective-permute-done.1.refs_1_, f32[8,128]{1,0:T(8,128)S(1)} %get-tuple-element.14.refs_2_, s32[1,61]{1,0:T(1,128)S(1)} %bitcast.5, s32[1,64]{1,0:T(1,128)S(1)} %bitcast.6, s32[1,10]{1,0:T(1,128)S(1)} %bitcast.7), custom_call_target="tpu_custom_call" | custom-call | tf_op jit(solution)/shard_map/pallas_call | solution.py:446
Async XLA Ops:
  87.7 3.6 %collective-permute-start = (f32[65,16,128]{2,1,0:T(8,128)S(1)}, f32[65,16,128]{2,1,0:T(8,128)S(1)}, u32[]{:S(2)}, u32[]{:S(2)}) collective-permute-start(f32[65,16,128]{2,1,0:T(8,128)S(1)} %shard_map.56.mine_ref), channel_id=1, source_target_pairs={{0,1},{1,0},{2,3},{3,2},{4,5},{5,4},{6,7},{7,6},{8,9},{9,8},{10,11... | collective-permute-start | bytes 1597448 | tf_op jit(solution)/shard_map/ppermute | solution.py:486
  91.3 7.9 %copy-start = (s32[61]{0:T(128)S(1)}, s32[61]{0:T(128)}, u32[]{:S(2)}) copy-start(s32[61]{0:T(128)} %param.7) | copy-start | bytes 736
  91.3 7.9 %copy-start.1 = (s32[64]{0:T(128)S(1)}, s32[64]{0:T(128)}, u32[]{:S(2)}) copy-start(s32[64]{0:T(128)} %param.9) | copy-start | bytes 772
  91.3 7.9 %copy-start.2 = (s32[10]{0:T(128)S(1)}, s32[10]{0:T(128)}, u32[]{:S(2)}) copy-start(s32[10]{0:T(128)} %param.8) | copy-start | bytes 124
  97.6 1.7 %collective-permute-start.1 = (f32[80,896]{1,0:T(8,128)S(1)}, f32[80,896]{1,0:T(8,128)S(1)}, u32[]{:S(2)}, u32[]{:S(2)}) collective-permute-start(f32[80,896]{1,0:T(8,128)S(1)} %get-tuple-element.13), channel_id=1, source_target_pairs={{0,1},{1,0},{2,3},{3,2},{4,5},{5,4},{6,7},{7,6},{8,9},{9,8},{10,11... | collective-permute-start | bytes 860168 | tf_op jit(solution)/shard_map/ppermute | solution.py:486

commit v6 on v4

--- a/solution.py
+++ b/solution.py
@@ -8,7 +8,7 @@
 TM = "tm"
 CORES = 2
 WEIGHTS = (1, 16, 4)
-DIGITS = ((3, 2, 1, 0), (3, 2, 1, 0), (2, 3, 0, 1))
+DIGITS = ((3, 2, 1, 0), (3, 2, 1, 0), (2, 1, 0, 3))
 PHASES = 6
 KCOUNT = 10
 USED = PHASES * KCOUNT

time: 101 us -> 101 us (level)
  no operation moved by 1% of the time
where the time goes in v6:
time: 101 us
  blocking collectives  84.5 us (84%)
  Pallas kernels  13.3 us (13%)
  starting transfers between devices  1.66 us (2%)
  waiting for transfers between devices  1.39 us (1%)
    all_to_all x1, blocking collectives, shards(): lax.all_to_all(pack(field, index), TM, 0, 0, axis_index_groups=groups, ti...  84.5 us
    pallas_call x1, Pallas kernels, spread(): pl.pallas_call(spread_kernel, in_specs=[VMEM] * 5, out_specs=[VMEM] * 3,...  6.23 us
    pallas_call x1, Pallas kernels, pack(): pl.pallas_call(pack_kernel, in_specs=[ANY] * 2, out_specs=VMEM, out_shape...  3.49 us
  transfers between devices with their start and end apart: 2, of which 1 were waited for; matrix products, arithmetic and copies ran while one was open for 0% of the time, Pallas kernels for 2%

profile of v6, /device:TPU:1, one launch (start us, length us, event | category | flops | bytes accessed | tf_op | source)
XLA Modules:
  0.0 100.9 jit_solution(15297841041858258690)
XLA Ops:
  0.0 3.5 %shard_map.55 = bf16[64,392,128]{2,1,0:T(8,128)(2,1)S(1)} custom-call(bf16[336,8192]{1,0:T(8,128)(2,1)} %field_ref.1, f32[10,336]{1,0:T(8,128)} %bitcast.8), custom_call_target="tpu_custom_call" | custom-call | tf_op jit(solution)/shard_map/pallas_call | solution.py:140
  3.5 84.5 %all_to_all.5.got_ref = bf16[64,392,128]{2,1,0:T(8,128)(2,1)S(1)} all-to-all(bf16[64,392,128]{2,1,0:T(8,128)(2,1)S(1)} %shard_map.55), channel_id=1, replica_groups={{118,110,102,126,86,78,70,94,54,46,38,62,22,14,6,30,116,108,100,124,84,..., dimensions={0} | all-to-all | bytes 12845056 | tf_op jit(solution)/shard_map/all_to_all | solution.py:481
  88.0 0.2 shard_map.56.mine_ref
  88.2 1.4 %collective-permute-start = (f32[65,16,128]{2,1,0:T(8,128)S(1)}, f32[65,16,128]{2,1,0:T(8,128)S(1)}, u32[]{:S(2)}, u32[]{:S(2)}) collective-permute-start(f32[65,16,128]{2,1,0:T(8,128)S(1)} %shard_map.56.mine_ref), channel_id=1, source_target_pairs={{0,1},{1,0},{2,3},{3,2},{4,5},{5,4},{6,7},{7,6},{8,9},{9,8},{10,11... | collective-permute-start | bytes 1597448 | tf_op jit(solution)/shard_map/ppermute | solution.py:487
  89.6 1.7 %shard_map.57 = (bf16[6,3584,128]{2,1,0:T(8,128)(2,1)S(1)}, f32[16,128]{1,0:T(8,128)S(1)}) custom-call(bf16[64,392,128]{2,1,0:T(8,128)(2,1)S(1)} %all_to_all.5.got_ref), custom_call_target="tpu_custom_call" | custom-call | tf_op jit(solution)/shard_map/pallas_call | solution.py:229
  91.3 0.0 collective-permute-done.other_ref
  91.3 0.0 copy-start
  91.3 0.0 copy-start.1
  91.3 0.0 copy-start.2
  91.3 6.2 %shard_map.58 = (f32[80,896]{1,0:T(8,128)S(1)}, f32[80,896]{1,0:T(8,128)S(1)}, f32[8,128]{1,0:T(8,128)S(1)}) custom-call(bf16[64,392,128]{2,1,0:T(8,128)(2,1)S(1)} %all_to_all.5.got_ref, f32[65,16,128]{2,1,0:T(8,128)S(1)} %shard_map.56.mine_ref, f32[65,16,128]{2,1,0:T(8,128)S(1)} %collective-permute-done.other_ref, ...), custom_call_target="tpu_custom_call" | custom-call | tf_op jit(solution)/shard_map/pallas_call | solution.py:374
  97.6 0.3 collective-permute-start.1
  97.8 1.4 %collective-permute-done.1.refs_1_ = f32[80,896]{1,0:T(8,128)S(1)} collective-permute-done((f32[80,896]{1,0:T(8,128)S(1)}, f32[80,896]{1,0:T(8,128)S(1)}, u32[]{:S(2)}, u32[]{:S(2)}) %collective-permute-start.1) | collective-permute-done | bytes 286752 | tf_op jit(solution)/shard_map/ppermute | solution.py:487
  99.2 0.0 copy-done
  99.2 0.0 copy-done.1
  99.2 0.0 copy-done.2
  99.2 1.7 %shard_map.59 = f32[10,64,61]{2,1,0:T(8,128)} custom-call(f32[80,896]{1,0:T(8,128)S(1)} %get-tuple-element.12.refs_0_, f32[80,896]{1,0:T(8,128)S(1)} %collective-permute-done.1.refs_1_, f32[8,128]{1,0:T(8,128)S(1)} %get-tuple-element.14.refs_2_, s32[1,61]{1,0:T(1,128)S(1)} %bitcast.5, s32[1,64]{1,0:T(1,128)S(1)} %bitcast.6, s32[1,10]{1,0:T(1,128)S(1)} %bitcast.7), custom_call_target="tpu_custom_call" | custom-call | tf_op jit(solution)/shard_map/pallas_call | solution.py:447
Async XLA Ops:
  88.2 3.1 %collective-permute-start = (f32[65,16,128]{2,1,0:T(8,128)S(1)}, f32[65,16,128]{2,1,0:T(8,128)S(1)}, u32[]{:S(2)}, u32[]{:S(2)}) collective-permute-start(f32[65,16,128]{2,1,0:T(8,128)S(1)} %shard_map.56.mine_ref), channel_id=1, source_target_pairs={{0,1},{1,0},{2,3},{3,2},{4,5},{5,4},{6,7},{7,6},{8,9},{9,8},{10,11... | collective-permute-start | bytes 1597448 | tf_op jit(solution)/shard_map/ppermute | solution.py:487
  91.3 7.9 %copy-start = (s32[61]{0:T(128)S(1)}, s32[61]{0:T(128)}, u32[]{:S(2)}) copy-start(s32[61]{0:T(128)} %param.7) | copy-start | bytes 736
  91.3 7.9 %copy-start.1 = (s32[64]{0:T(128)S(1)}, s32[64]{0:T(128)}, u32[]{:S(2)}) copy-start(s32[64]{0:T(128)} %param.9) | copy-start | bytes 772
  91.3 7.9 %copy-start.2 = (s32[10]{0:T(128)S(1)}, s32[10]{0:T(128)}, u32[]{:S(2)}) copy-start(s32[10]{0:T(128)} %param.8) | copy-start | bytes 124
  97.6 1.7 %collective-permute-start.1 = (f32[80,896]{1,0:T(8,128)S(1)}, f32[80,896]{1,0:T(8,128)S(1)}, u32[]{:S(2)}, u32[]{:S(2)}) collective-permute-start(f32[80,896]{1,0:T(8,128)S(1)} %get-tuple-element.13), channel_id=1, source_target_pairs={{0,1},{1,0},{2,3},{3,2},{4,5},{5,4},{6,7},{7,6},{8,9},{9,8},{10,11... | collective-permute-start | bytes 860168 | tf_op jit(solution)/shard_map/ppermute | solution.py:487
